TPU v7x, 128 devices: a whole 4x4x4 slice. The times are simulated.
128 devices in a mesh: ctx: 16 (over y, z), wt: 8 (over x, core).
Axes of the slice: x: 4, y: 4, z: 4, core: 2. Of those that a mesh axis runs over, the one named last changes fastest.
Arguments:
- frames: bfloat16 [1024, 1280], P('wt'), may hold values from -6 to 6
- span_source: int32 [64], P('wt'), may hold values from 0 to 7, as said below
- adapter_weight: bfloat16 [1280, 4096], P(None, 'ctx'), may hold values from -0.15625 to 0.15625
- adapter_bias: float32 [4096], P('ctx'), may hold values from -3 to 3
- norm_gain: float32 [4096], replicated, may hold values from 0.25 to 1.75
- qkv_weight: bfloat16 [4096, 3, 4096], P('wt', None, 'ctx'), may hold values from -0.09375 to 0.09375
- out_weight: bfloat16 [4096, 4096], P('ctx', 'wt'), may hold values from -0.125 to 0.125
- k_cache: bfloat16 [16, 2048, 4096], P('wt', 'ctx'), may hold values from -600 to 600
- v_cache: bfloat16 [16, 2048, 4096], P('wt', 'ctx'), may hold values from -12 to 12
- lengths: int32 [16], P('wt'), may hold values from 1 to 2048
Outputs:
- attn_out: bfloat16 [1024, 4096], P('wt', 'ctx')
- new_keys: bfloat16 [1024, 4096], P('wt', 'ctx')
- new_values: bfloat16 [1024, 4096], P('wt', 'ctx')
Inputs may be any that keep to these rules, and one draw needn't show every extreme that they name: `span_source`: each aligned block of 8 entries is a permutation of 0 to 7.
All inputs are finite; a program needn't handle non-finite values.
Results may differ from a plain program's by a relative error of at most 0.02.
Values may be sent and summed in bfloat16 or wider, within the bound.
No kernel may reach another device: no remote copies, remote signals or barrier semaphores. Data moves between devices by JAX's collectives and lax.ppermute only.
A program may use at most 64 MiB of HBM per device.

v0:
```python
import jax
import jax.numpy as jnp
from jax import lax
from jax.sharding import PartitionSpec as P

HEADS = 32
HEAD = 128
FLOOR_SCORE = -1e30


def in_order(blocks, dim):
    lengths = list(blocks.shape[1:])
    lengths[dim] *= blocks.shape[0]
    return jnp.moveaxis(blocks, 0, dim).reshape(lengths)


def from_everyone(x, axis):
    count = lax.axis_size(axis)
    return lax.all_to_all(jnp.broadcast_to(x[None], (count, *x.shape)), axis, 0, 0, tiled=True)


def gather_directly(x, axis, dim):
    return in_order(from_everyone(x, axis), dim)


def cut_along(x, dim, count):
    before, after = (x.shape[:dim], x.shape[dim + 1 :])
    return jnp.moveaxis(x.reshape(*before, count, -1, *after), dim, 0)


def summed_on_arrival(x, axis, dim):
    count = lax.axis_size(axis)
    blocks = lax.all_to_all(cut_along(x, dim, count), axis, 0, 0, tiled=True)
    return jnp.sum(blocks.astype(jnp.float32), axis=0)


def rotate(values, positions):
    half = values.shape[-1] // 2
    freq = 10000.0 ** (-2.0 * jnp.arange(half, dtype=jnp.float32) / values.shape[-1])
    angle = positions.astype(jnp.float32)[:, None] * freq[None, :]
    cosine = jnp.cos(angle)[:, None, :]
    sine = jnp.sin(angle)[:, None, :]
    first = values[..., :half]
    second = values[..., half:]
    return jnp.concatenate(
        [first * cosine - second * sine, second * cosine + first * sine], axis=-1
    )


def combine_parts(left, right):
    left_max, left_total, left_numer = left
    right_max, right_total, right_numer = right
    joint = jnp.maximum(left_max, right_max)
    left_scale = jnp.exp(left_max - joint)
    right_scale = jnp.exp(right_max - joint)
    return (
        joint,
        left_total * left_scale + right_total * right_scale,
        left_numer * left_scale[..., None] + right_numer * right_scale[..., None],
    )


def finish_heads(parts):
    shard_max, shard_total, shard_numer = parts
    joint = jnp.max(shard_max, axis=0)
    factor = jnp.exp(shard_max - joint[None])
    total = jnp.sum(shard_total * factor, axis=0)
    numer = jnp.sum(shard_numer * factor[..., None], axis=0)
    return (numer / total[..., None]).astype(jnp.bfloat16)


def shards(
    frames,
    span_source,
    adapter_weight,
    adapter_bias,
    norm_gain,
    qkv_weight,
    out_weight,
    k_cache,
    v_cache,
    lengths,
):
    tok_rows, audio_width = frames.shape
    group_spans = span_source.shape[0]
    span_len = tok_rows // group_spans
    meet_count = lengths.shape[0]
    new_count = tok_rows // meet_count
    hist_local = k_cache.shape[1]
    cols_local = qkv_weight.shape[2]
    heads_here = cols_local // HEAD
    scale = HEAD ** (-0.5)
    ctx_rank = lax.axis_index("ctx")
    head_start = ctx_rank * heads_here
    ordered = frames.reshape(group_spans, span_len, audio_width)[span_source].reshape(
        tok_rows, audio_width
    )
    adapted = (
        jnp.dot(ordered, adapter_weight, preferred_element_type=jnp.float32) + adapter_bias
    ).astype(jnp.bfloat16)
    features = gather_directly(adapted, "ctx", 1)
    wide = features.astype(jnp.float32)
    normed = (
        wide * lax.rsqrt(jnp.mean(wide * wide, axis=-1, keepdims=True) + 1e-06) * norm_gain
    ).astype(jnp.bfloat16)
    qkv_full, out_rows = (
        lax.all_gather(qkv_weight, "wt", axis=0, tiled=True),
        lax.all_gather(out_weight, "wt", axis=1, tiled=True),
    )
    projected = jnp.einsum("rd,dke->rke", normed, qkv_full, preferred_element_type=jnp.float32)
    positions = (lengths[:, None] + jnp.arange(new_count, dtype=jnp.int32)[None, :]).reshape(
        tok_rows
    )
    query_local = rotate(projected[:, 0].reshape(tok_rows, heads_here, HEAD), positions).astype(
        jnp.bfloat16
    )
    key_local = rotate(projected[:, 1].reshape(tok_rows, heads_here, HEAD), positions).astype(
        jnp.bfloat16
    )
    value_local = projected[:, 2].reshape(tok_rows, heads_here, HEAD).astype(jnp.bfloat16)
    query_every = gather_directly(query_local.reshape(tok_rows, cols_local), "ctx", 1)
    query_heads = query_every.reshape(meet_count, new_count, HEADS, HEAD)
    keys_hist = k_cache.reshape(meet_count, hist_local, HEADS, HEAD)
    vals_hist = v_cache.reshape(meet_count, hist_local, HEADS, HEAD)
    scores = (
        jnp.einsum("mthd,mphd->mhtp", query_heads, keys_hist, preferred_element_type=jnp.float32)
        * scale
    )
    key_place = ctx_rank * hist_local + jnp.arange(hist_local, dtype=jnp.int32)
    live = (key_place[None, :] < lengths[:, None])[:, None, None, :]
    hist_max = jnp.maximum(jnp.max(jnp.where(live, scores, -jnp.inf), axis=-1), FLOOR_SCORE)
    hist_weights = jnp.where(live, jnp.exp(scores - hist_max[..., None]), 0.0)
    hist_total = jnp.sum(hist_weights, axis=-1)
    hist_numer = jnp.einsum(
        "mhtp,mphd->mthd",
        hist_weights.astype(jnp.bfloat16),
        vals_hist,
        preferred_element_type=jnp.float32,
    ).reshape(tok_rows, HEADS, HEAD)
    hist_max = jnp.transpose(hist_max, (0, 2, 1)).reshape(tok_rows, HEADS)
    hist_total = jnp.transpose(hist_total, (0, 2, 1)).reshape(tok_rows, HEADS)
    query_new = query_local.reshape(meet_count, new_count, heads_here, HEAD)
    key_new = key_local.reshape(meet_count, new_count, heads_here, HEAD)
    value_new = value_local.reshape(meet_count, new_count, heads_here, HEAD)
    new_scores = (
        jnp.einsum("mthd,mshd->mhts", query_new, key_new, preferred_element_type=jnp.float32)
        * scale
    )
    causal = (
        jnp.arange(new_count, dtype=jnp.int32)[:, None]
        >= jnp.arange(new_count, dtype=jnp.int32)[None, :]
    )[None, None]
    new_max = jnp.max(jnp.where(causal, new_scores, -jnp.inf), axis=-1)
    new_weights = jnp.where(causal, jnp.exp(new_scores - new_max[..., None]), 0.0)
    new_total = jnp.sum(new_weights, axis=-1)
    new_numer = jnp.einsum(
        "mhts,mshd->mthd",
        new_weights.astype(jnp.bfloat16),
        value_new,
        preferred_element_type=jnp.float32,
    ).reshape(tok_rows, heads_here, HEAD)
    new_max = jnp.transpose(new_max, (0, 2, 1)).reshape(tok_rows, heads_here)
    new_total = jnp.transpose(new_total, (0, 2, 1)).reshape(tok_rows, heads_here)
    own_part = (
        lax.dynamic_slice_in_dim(hist_max, head_start, heads_here, 1),
        lax.dynamic_slice_in_dim(hist_total, head_start, heads_here, 1),
        lax.dynamic_slice_in_dim(hist_numer, head_start, heads_here, 1),
    )
    joined_max, joined_total, joined_numer = combine_parts(
        own_part, (new_max, new_total, new_numer)
    )
    part_max = lax.dynamic_update_slice_in_dim(hist_max, joined_max, head_start, 1)
    part_total = lax.dynamic_update_slice_in_dim(hist_total, joined_total, head_start, 1)
    part_numer = lax.dynamic_update_slice_in_dim(hist_numer, joined_numer, head_start, 1)
    attended = finish_heads(
        (
            lax.all_to_all(
                part_max[None].astype(jnp.bfloat16), "ctx", split_axis=2, concat_axis=0, tiled=True
            ).astype(jnp.float32),
            lax.all_to_all(
                part_total[None].astype(jnp.bfloat16),
                "ctx",
                split_axis=2,
                concat_axis=0,
                tiled=True,
            ).astype(jnp.float32),
            lax.all_to_all(
                part_numer[None].astype(jnp.bfloat16),
                "ctx",
                split_axis=2,
                concat_axis=0,
                tiled=True,
            ).astype(jnp.float32),
        )
    )
    attended_flat = attended.reshape(tok_rows, cols_local)
    out_terms = jnp.dot(attended_flat, out_rows, preferred_element_type=jnp.float32)
    attn_out = summed_on_arrival(out_terms.astype(jnp.bfloat16), "ctx", 1).astype(jnp.bfloat16)
    return (
        attn_out,
        key_local.reshape(tok_rows, cols_local),
        value_local.reshape(tok_rows, cols_local),
    )


def solution(mesh):
    return jax.shard_map(
        shards,
        mesh=mesh,
        in_specs=(
            P("wt", None),
            P("wt"),
            P(None, "ctx"),
            P("ctx"),
            P(),
            P("wt", None, "ctx"),
            P("ctx", "wt"),
            P("wt", "ctx", None),
            P("wt", "ctx", None),
            P("wt"),
        ),
        out_specs=(P("wt", "ctx"), P("wt", "ctx"), P("wt", "ctx")),
        check_vma=False,
    )
```

profile of v0, /device:TPU:0, one launch (start us, length us, event | category | flops | bytes accessed | tf_op | source)
XLA Modules:
  0.0 184.5 jit_solution(12653421119872062903)
XLA Ops:
  7.2 0.7 all-gather.3.cloned.1.call-update
  7.9 0.7 compare_select_fusion
  8.6 1.5 gather_fusion
  10.1 1.4 fusion.14
  11.5 1.1 broadcast_in_dim.95
  12.6 8.2 %all-to-all-start = ((bf16[16,128,256]{2,1,0:T(8,128)(2,1)}), bf16[16,128,256]{2,1,0:T(8,128)(2,1)}, u32[]{:S(2)}, u32[]{:S(2)}) async-start(bf16[16,128,256]{2,1,0:T(8,128)(2,1)} %broadcast_in_dim.95), calls=%async_computation | async-start | bytes 2097152 | tf_op jit(solution)/shard_map/all_to_all | solution.py:19
  20.8 0.7 all-gather.5.cloned.1.call-update
  21.9 16.7 %all-to-all-done = bf16[16,128,256]{2,1,0:T(8,128)(2,1)} async-done(((bf16[16,128,256]{2,1,0:T(8,128)(2,1)}), bf16[16,128,256]{2,1,0:T(8,128)(2,1)}, u32[]{:S(2)}, u32[]{:S(2)}) %all-to-all-start) | async-done | bytes 1048608 | tf_op jit(solution)/shard_map/all_to_all | solution.py:19
  38.6 1.6 copy.143
  40.8 1.5 fusion.8
  42.3 10.7 %all-gather.3.cloned.1.call-done = bf16[4096,3,256]{2,0,1:T(8,128)(2,1)} async-done(((bf16[512,3,256]{2,0,1:T(8,128)(2,1)}), bf16[4096,3,256]{2,0,1:T(8,128)(2,1)}) %all-gather.3.cloned.1.call-update) | async-done | bytes 6291472 | tf_op jit(solution)/shard_map/all_gather | solution.py:107
  53.0 4.2 %fusion.16 = f32[128,3,256]{2,0,1:T(8,128)S(1)} fusion(bf16[4096,3,256]{2,0,1:T(8,128)(2,1)} %all-gather.3.cloned.1.call-done, bf16[128,4096]{0,1:T(8,128)(2,1)} %fusion.8), kind=kOutput, calls=%fused_computation.24 | convolution fusion | flops 805306368 | bytes 7733248 | tf_op jit(solution)/shard_map/rd,dke->rke/dot_general | solution.py:110
  58.1 0.6 pad_maximum_fusion
  58.8 1.1 broadcast_in_dim.96
  59.9 7.0 %all-to-all-start.1 = ((bf16[16,128,256]{2,1,0:T(8,128)(2,1)}), bf16[16,128,256]{2,1,0:T(8,128)(2,1)S(1)}, u32[]{:S(2)}, u32[]{:S(2)}) async-start(bf16[16,128,256]{2,1,0:T(8,128)(2,1)} %broadcast_in_dim.96), calls=%async_computation.1 | async-start | bytes 2097152 | tf_op jit(solution)/shard_map/all_to_all | solution.py:19
  66.9 0.7 broadcast_compare_fusion
  67.6 1.5 concatenate.25
  69.0 1.5 concatenate.26
  70.5 1.5 concatenate.28
  72.0 1.5 concatenate.29
  73.4 1.6 copy.155
  75.0 1.6 copy.156
  76.5 1.6 copy.159
  78.1 1.6 copy.160
  79.7 1.8 select_reduce_fusion.1
  81.5 0.6 slice.46
  82.7 0.8 reshape.231
  83.5 1.0 fusion.24
  85.0 1.3 reshape.234
  86.3 1.5 convert_element_type.128
  87.8 1.2 convolution_bitcast_fusion
  89.0 0.7 copy.165
  89.7 1.6 copy.148
  91.2 1.4 reshape_reshape.3
  92.7 2.9 %select_reduce_fusion = (f32[2,32,64]{2,1,0:T(8,128)S(1)}, f32[2,32,64,128]{3,2,1,0:T(8,128)}) fusion(pred[2,128]{1,0:T(4,128)(4,1)S(1)} %copy-done.9, bf16[2,64,32,128]{3,2,1,0:T(8,128)(2,1)S(1)} %reshape_reshape.3, bf16[2,128,4096]{2,1,0:T(8,128)(2,1)S(1)} %copy-done), kind=kOutput, calls=%fused_computation.14 | convolution fusion | flops 135786496 | bytes 5259520 | tf_op jit(solution)/shard_map/mthd,mphd->mhtp/dot_general | solution.py:126
  95.8 2.5 %fusion.12 = f32[2,32,64]{2,1,0:T(8,128)S(1)} fusion(f32[2,32,64,128]{3,2,1,0:T(8,128)} %get-tuple-element.21, f32[2,32,64]{2,1,0:T(8,128)S(1)} %get-tuple-element.15, pred[2,128]{1,0:T(4,128)(4,1)S(1)} %copy-done.9), kind=kLoop, calls=%fused_computation.17 | loop fusion | flops 2093056 | bytes 2130176 | tf_op jit(solution)/shard_map/reduce_sum | solution.py:133
  98.5 0.6 copy.219
  99.2 7.2 %all-to-all-start.3 = ((bf16[16,2,128]{2,1,0:T(2,128)(2,1)}), bf16[16,2,128]{2,1,0:T(2,128)(2,1)S(1)}, u32[]{:S(2)}, u32[]{:S(2)}) async-start(bf16[16,2,128]{2,1,0:T(2,128)(2,1)} %bitcast.125), calls=%async_computation.3 | async-start | bytes 16384 | tf_op jit(solution)/shard_map/all_to_all | solution.py:177
  106.4 4.3 %fusion.9 = f32[2,64,32,128]{3,1,2,0:T(8,128)} fusion(f32[2,32,64,128]{3,2,1,0:T(8,128)} %get-tuple-element.21, f32[2,32,64]{2,1,0:T(8,128)S(1)} %get-tuple-element.15, pred[2,128]{1,0:T(4,128)(4,1)S(1)} %copy-done.9, bf16[2,128,4096]{2,1,0:T(8,128)(2,1)} %param.18), kind=kOutput, calls=%fused_computation.16 | convolution fusion | flops 136314880 | bytes 6308096 | tf_op jit(solution)/shard_map/mhtp,mphd->mthd/dot_general | solution.py:134
  110.7 0.6 copy.218
  111.5 2.8 %copy.152 = f32[2,64,32,128]{3,2,1,0:T(8,128)S(1)} copy(f32[2,64,32,128]{3,1,2,0:T(8,128)} %fusion.9) | data formatting | bytes 4194304 | tf_op jit(solution)/shard_map/mhtp,mphd->mthd/transpose | solution.py:134
  114.4 1.3 copy-done.1
  115.7 1.3 copy.221
  117.0 7.2 %all-to-all-start.4 = ((bf16[16,2,128]{2,1,0:T(2,128)(2,1)}), bf16[16,2,128]{2,1,0:T(2,128)(2,1)S(1)}, u32[]{:S(2)}, u32[]{:S(2)}) async-start(bf16[16,2,128]{2,1,0:T(2,128)(2,1)} %bitcast.124), calls=%async_computation.4 | async-start | bytes 16384 | tf_op jit(solution)/shard_map/all_to_all | solution.py:180
  124.2 2.0 %bitcast_dynamic-update-slice_fusion = f32[1,128,32,128]{3,2,1,0:T(8,128)} fusion(f32[1,128,32,128]{3,2,1,0:T(8,128)} %copy.221, s32[]{:T(128)S(6)} %select_n.28, f32[128,2,128]{2,0,1:T(8,128)S(1)} %bitcast.133, f32[128,32,128]{2,1,0:T(8,128)} %bitcast.127, f32[128,2]{1,0:T(8,128)S(1)} %copy.166, f32[128,2]{1,0:T(8,128)S(1)} %copy.162), kind=kLoop, calls=%fused_computation.32 | loop fusion | flops 98304 | bytes 395268 | tf_op jit(solution)/shard_map/dynamic_update_slice | solution.py:174
  126.3 1.8 convert_element_type.130
  128.1 1.4 copy.168
  129.5 2.3 %all-to-all-done.4 = bf16[16,2,128]{2,1,0:T(2,128)(2,1)S(1)} async-done(((bf16[16,2,128]{2,1,0:T(2,128)(2,1)}), bf16[16,2,128]{2,1,0:T(2,128)(2,1)S(1)}, u32[]{:S(2)}, u32[]{:S(2)}) %all-to-all-start.4) | async-done | bytes 8224 | tf_op jit(solution)/shard_map/all_to_all | solution.py:180
  131.7 5.0 %all-to-all-start.2 = ((bf16[1,128,32,128]{3,1,0,2:T(8,128)(2,1)}), bf16[1,128,32,128]{3,1,0,2:T(8,128)(2,1)S(1)}, u32[]{:S(2)}, u32[]{:S(2)}) async-start(bf16[1,128,32,128]{3,1,0,2:T(8,128)(2,1)} %copy.168), calls=%async_computation.2 | async-start | bytes 2097152 | tf_op jit(solution)/shard_map/all_to_all | solution.py:187
  136.8 0.6 reshape.253
  137.4 0.7 copy.185
  138.7 1.2 reduce_max.35
  139.9 0.6 reshape.255
  140.5 0.7 copy.175
  141.2 1.3 fusion.37
  142.5 10.1 %all-to-all-done.2 = bf16[1,128,32,128]{3,1,0,2:T(8,128)(2,1)S(1)} async-done(((bf16[1,128,32,128]{3,1,0,2:T(8,128)(2,1)}), bf16[1,128,32,128]{3,1,0,2:T(8,128)(2,1)S(1)}, u32[]{:S(2)}, u32[]{:S(2)}) %all-to-all-start.2) | async-done | bytes 1048608 | tf_op jit(solution)/shard_map/all_to_all | solution.py:187
  152.6 1.4 fusion.6
  154.3 2.1 %convolution_convert_fusion = bf16[128,4096]{1,0:T(8,128)(2,1)S(1)} fusion(bf16[128,256]{0,1:T(8,128)(2,1)S(1)} %bitcast.137, bf16[256,4096]{1,0:T(8,128)(2,1)} %all-gather.5.cloned.1.call-done), kind=kOutput, calls=%fused_computation.1 | convolution fusion | flops 268959744 | bytes 3211264 | tf_op jit(solution)/shard_map/dot_general | solution.py:197
  156.4 1.1 copy.215
  157.5 3.7 %all-to-all-start.5 = ((bf16[16,128,256]{2,1,0:T(8,128)(2,1)}), bf16[16,128,256]{2,1,0:T(8,128)(2,1)S(1)}, u32[]{:S(2)}, u32[]{:S(2)}) async-start(bf16[16,128,256]{2,1,0:T(8,128)(2,1)} %bitcast.131), calls=%async_computation.5 | async-start | bytes 2097152 | tf_op jit(solution)/shard_map/all_to_all | solution.py:33
  161.1 1.6 copy.182
  162.7 0.6 slice_bitcast_fusion
  163.3 13.6 %all-to-all-done.5 = bf16[16,128,256]{2,1,0:T(8,128)(2,1)S(1)} async-done(((bf16[16,128,256]{2,1,0:T(8,128)(2,1)}), bf16[16,128,256]{2,1,0:T(8,128)(2,1)S(1)}, u32[]{:S(2)}, u32[]{:S(2)}) %all-to-all-start.5) | async-done | bytes 1048608 | tf_op jit(solution)/shard_map/all_to_all | solution.py:33
  176.9 0.8 reduce_sum.62
  (58 shorter events, 4.7 us)
Async XLA Ops:
  7.2 85.5 %copy-start = (bf16[2,128,4096]{2,1,0:T(8,128)(2,1)S(1)}, bf16[2,128,4096]{2,1,0:T(8,128)(2,1)}, u32[]{:S(2)}) copy-start(bf16[2,128,4096]{2,1,0:T(8,128)(2,1)} %param.17) | copy-start | bytes 6291460
  7.2 45.8 %all-gather.3.cloned.1.call-start = ((), (), s32[]{:S(2)}) async-start(), calls=%async_computation.6 | async-start | bytes 7077888 | tf_op jit(solution)/shard_map/all_gather | solution.py:107
  10.1 11.4 %copy-start.10 = (s32[2]{0:T(128)S(1)}, s32[2]{0:T(128)}, u32[]{:S(2)}) copy-start(s32[2]{0:T(128)} %param.19) | copy-start | bytes 28
  12.6 26.0 %all-to-all-start = ((bf16[16,128,256]{2,1,0:T(8,128)(2,1)}), bf16[16,128,256]{2,1,0:T(8,128)(2,1)}, u32[]{:S(2)}, u32[]{:S(2)}) async-start(bf16[16,128,256]{2,1,0:T(8,128)(2,1)} %broadcast_in_dim.95), calls=%async_computation | async-start | bytes 2097152 | tf_op jit(solution)/shard_map/all_to_all | solution.py:19
  20.8 20.0 %copy-start.7 = (f32[4096]{0:T(1024)S(1)}, f32[4096]{0:T(1024)}, u32[]{:S(2)}) copy-start(f32[4096]{0:T(1024)} %param.14) | copy-start | bytes 49156
  20.8 133.5 %all-gather.5.cloned.1.call-start = ((), (), s32[]{:S(2)}) async-start(), calls=%async_computation.7 | async-start | bytes 2359296 | tf_op jit(solution)/shard_map/all_gather | solution.py:108
  57.5 0.6 copy-start.3
  57.5 1.2 copy-start.4
  57.5 1.2 copy-start.5
  57.5 1.2 copy-start.6
  59.9 29.8 %all-to-all-start.1 = ((bf16[16,128,256]{2,1,0:T(8,128)(2,1)}), bf16[16,128,256]{2,1,0:T(8,128)(2,1)S(1)}, u32[]{:S(2)}, u32[]{:S(2)}) async-start(bf16[16,128,256]{2,1,0:T(8,128)(2,1)} %broadcast_in_dim.96), calls=%async_computation.1 | async-start | bytes 2097152 | tf_op jit(solution)/shard_map/all_to_all | solution.py:19
  89.7 3.0 %copy-start.9 = (pred[2,128]{1,0:T(4,128)(4,1)S(1)}, pred[2,128]{1,0:T(4,128)(4,1)}, u32[]{:S(2)}) copy-start(pred[2,128]{1,0:T(4,128)(4,1)} %broadcast_compare_fusion) | copy-start | bytes 772
  99.2 17.9 %all-to-all-start.3 = ((bf16[16,2,128]{2,1,0:T(2,128)(2,1)}), bf16[16,2,128]{2,1,0:T(2,128)(2,1)S(1)}, u32[]{:S(2)}, u32[]{:S(2)}) async-start(bf16[16,2,128]{2,1,0:T(2,128)(2,1)} %bitcast.125), calls=%async_computation.3 | async-start | bytes 16384 | tf_op jit(solution)/shard_map/all_to_all | solution.py:177
  106.4 4.3 %copy-start.8 = (f32[128,2]{0,1:T(2,128)S(1)}, f32[128,2]{0,1:T(2,128)}, u32[]{:S(2)}) copy-start(f32[128,2]{0,1:T(2,128)} %reshape.234) | copy-start | bytes 3076
  114.4 1.3 copy-start.1
  115.7 8.6 %copy-start.2 = (f32[2,64,2,128]{3,1,0,2:T(8,128)S(1)}, f32[2,64,2,128]{3,1,0,2:T(8,128)}, u32[]{:S(2)}) copy-start(f32[2,64,2,128]{3,1,0,2:T(8,128)} %copy.165) | copy-start | bytes 393220
  117.0 14.7 %all-to-all-start.4 = ((bf16[16,2,128]{2,1,0:T(2,128)(2,1)}), bf16[16,2,128]{2,1,0:T(2,128)(2,1)S(1)}, u32[]{:S(2)}, u32[]{:S(2)}) async-start(bf16[16,2,128]{2,1,0:T(2,128)(2,1)} %bitcast.124), calls=%async_computation.4 | async-start | bytes 16384 | tf_op jit(solution)/shard_map/all_to_all | solution.py:180
  131.7 20.9 %all-to-all-start.2 = ((bf16[1,128,32,128]{3,1,0,2:T(8,128)(2,1)}), bf16[1,128,32,128]{3,1,0,2:T(8,128)(2,1)S(1)}, u32[]{:S(2)}, u32[]{:S(2)}) async-start(bf16[1,128,32,128]{3,1,0,2:T(8,128)(2,1)} %copy.168), calls=%async_computation.2 | async-start | bytes 2097152 | tf_op jit(solution)/shard_map/all_to_all | solution.py:187
  157.5 19.5 %all-to-all-start.5 = ((bf16[16,128,256]{2,1,0:T(8,128)(2,1)}), bf16[16,128,256]{2,1,0:T(8,128)(2,1)S(1)}, u32[]{:S(2)}, u32[]{:S(2)}) async-start(bf16[16,128,256]{2,1,0:T(8,128)(2,1)} %bitcast.131), calls=%async_computation.5 | async-start | bytes 2097152 | tf_op jit(solution)/shard_map/all_to_all | solution.py:33
Sparse Core Ops, SparseCore 0:
  9.7 43.2 all-gather.2
  54.7 25.3 all-gather.4
where the time goes:
time: 186 us; the launch traced here: 185 us
  waiting for transfers between devices  54.7 us (29%)
  local copies, waits for them, and re-layouts  42.2 us (23%)
  starting transfers between devices  38.4 us (21%)
  matrix products  17.7 us (10%)
  other arithmetic  17.1 us (9%)
  between operations  14.4 us (8%)
    all_to_all x2, waiting for transfers between devices, from_everyone(): lax.all_to_all(jnp.broadcast_to(x[None], (count, *x.shape)), axis, 0, 0,...  16.7 us
    all_to_all x2, starting transfers between devices, from_everyone(): lax.all_to_all(jnp.broadcast_to(x[None], (count, *x.shape)), axis, 0, 0,...  15.2 us
    all_to_all x1, waiting for transfers between devices, summed_on_arrival(): blocks = lax.all_to_all(cut_along(x, dim, count), axis, 0, 0, tiled=True)  13.6 us
    concatenate x8, local copies, waits for them, and re-layouts, rotate(): jnp.concatenate([first * cosine - second * sine, second * cosine + first...  12.1 us
    all_gather x1, waiting for transfers between devices, shards(): lax.all_gather(qkv_weight, 'wt', axis=0, tiled=True)  10.7 us
    all_to_all x1, waiting for transfers between devices, shards(): lax.all_to_all(part_numer[None].astype(jnp.bfloat16), 'ctx', split_axis=2...  10.1 us
    all_to_all x1, starting transfers between devices, shards(): lax.all_to_all(part_total[None].astype(jnp.bfloat16), 'ctx', split_axis=2...  7.21 us
    all_to_all x1, starting transfers between devices, shards(): lax.all_to_all(part_max[None].astype(jnp.bfloat16), 'ctx', split_axis=2,...  7.21 us
  transfers between devices with their start and end apart: 8, of which 5 were waited for; matrix products, arithmetic and copies ran while one was open for 39% of the time, Pallas kernels for 0%

commit v1 on v0

--- a/solution.py
+++ b/solution.py
@@ -104,7 +104,9 @@
         wide * lax.rsqrt(jnp.mean(wide * wide, axis=-1, keepdims=True) + 1e-06) * norm_gain
     ).astype(jnp.bfloat16)
     qkv_full, out_rows = (
-        lax.all_gather(qkv_weight, "wt", axis=0, tiled=True),
+        jnp.concatenate(
+            lax.all_to_all(jnp.stack([qkv_weight] * lax.axis_size("wt")), "wt", 0, 0), axis=0
+        ),
         lax.all_gather(out_weight, "wt", axis=1, tiled=True),
     )
     projected = jnp.einsum("rd,dke->rke", normed, qkv_full, preferred_element_type=jnp.float32)

time: 186 us -> 255 us (1.37)
  waiting for transfers between devices: 54.7 us -> 101 us
  blocking collectives: 0 us -> 24.9 us
  starting transfers between devices: 38.4 us -> 31.9 us
  local copies, waits for them, and re-layouts: 42.2 us -> 47.8 us
  matrix products: 17.7 us -> 14.8 us
    all_to_all x0 -> x1, waiting for transfers between devices: none -> 75.1 us  [shards(): lax.all_to_all(jnp.stack([qkv_weight] * lax.axis_size('wt')), 'wt', 0, 0)]
    all_to_all x0 -> x1, blocking collectives: none -> 24.9 us  [from_everyone(): lax.all_to_all(jnp.broadcast_to(x[None], (count, *x.shape)), axis, 0, 0,...]
    all_to_all x2 -> x1, waiting for transfers between devices: 16.7 us -> 0.01 us  [from_everyone(): lax.all_to_all(jnp.broadcast_to(x[None], (count, *x.shape)), axis, 0, 0,...]
    all_to_all x2 -> x1, starting transfers between devices: 15.2 us -> 3.85 us  [from_everyone(): lax.all_to_all(jnp.broadcast_to(x[None], (count, *x.shape)), axis, 0, 0,...]
    all_gather x1 -> x0, waiting for transfers between devices: 10.7 us -> none  [shards(): lax.all_gather(qkv_weight, 'wt', axis=0, tiled=True)]
    all_to_all x0 -> x1, starting transfers between devices: none -> 4.87 us  [shards(): lax.all_to_all(jnp.stack([qkv_weight] * lax.axis_size('wt')), 'wt', 0, 0)]
    another operation x0 -> x1, local copies, waits for them, and re-layouts: none -> 3.33 us  [shards(): jnp.stack([qkv_weight] * lax.axis_size('wt'))]
    all_to_all x0 -> x1, local copies, waits for them, and re-layouts: none -> 3.2 us  [shards(): lax.all_to_all(jnp.stack([qkv_weight] * lax.axis_size('wt')), 'wt', 0, 0)]
  transfers between devices with their start and end apart: 8 -> 7, of which waited for: 5 -> 4; matrix products, arithmetic and copies ran while one was open for 39% -> 27% of each run, Pallas kernels for 0% -> 0%
where the time goes in v1:
time: 255 us; the launch traced here: 254 us
  waiting for transfers between devices  101 us (40%)
  local copies, waits for them, and re-layouts  47.8 us (19%)
  starting transfers between devices  31.9 us (13%)
  blocking collectives  24.9 us (10%)
  other arithmetic  18.6 us (7%)
  matrix products  14.8 us (6%)
  between operations  14.4 us (6%)
    all_to_all x1, waiting for transfers between devices, shards(): lax.all_to_all(jnp.stack([qkv_weight] * lax.axis_size('wt')), 'wt', 0, 0)  75.1 us
    all_to_all x1, blocking collectives, from_everyone(): lax.all_to_all(jnp.broadcast_to(x[None], (count, *x.shape)), axis, 0, 0,...  24.9 us
    all_to_all x1, waiting for transfers between devices, summed_on_arrival(): blocks = lax.all_to_all(cut_along(x, dim, count), axis, 0, 0, tiled=True)  13.7 us
    concatenate x8, local copies, waits for them, and re-layouts, rotate(): jnp.concatenate([first * cosine - second * sine, second * cosine + first...  12.2 us
    all_to_all x1, waiting for transfers between devices, shards(): lax.all_to_all(part_numer[None].astype(jnp.bfloat16), 'ctx', split_axis=2...  9.43 us
    all_to_all x1, starting transfers between devices, shards(): lax.all_to_all(part_total[None].astype(jnp.bfloat16), 'ctx', split_axis=2...  7.21 us
    all_to_all x1, starting transfers between devices, shards(): lax.all_to_all(part_max[None].astype(jnp.bfloat16), 'ctx', split_axis=2,...  7.21 us
    unnamed x32, local copies, waits for them, and re-layouts  6.43 us
  transfers between devices with their start and end apart: 7, of which 4 were waited for; matrix products, arithmetic and copies ran while one was open for 27% of the time, Pallas kernels for 0%

profile of v1, /device:TPU:0, one launch (start us, length us, event | category | flops | bytes accessed | tf_op | source)
XLA Modules:
  0.0 253.6 jit_solution(15471865690593958988)
XLA Ops:
  7.2 0.8 compare_select_fusion
  8.0 1.5 gather_fusion
  9.6 1.4 fusion.15
  11.1 24.9 %all_to_all.53 = bf16[16,128,256]{2,1,0:T(8,128)(2,1)} all-to-all(bf16[16,128,256]{2,1,0:T(8,128)(2,1)S(1)} %broadcast_in_dim.95), channel_id=1, replica_groups=mesh['ctx'=16,'wt'=8] {'ctx'}, dimensions={0} | all-to-all | bytes 2097152 | tf_op jit(solution)/shard_map/all_to_all | solution.py:19
  36.0 3.3 %stack.2 = bf16[8,512,3,256]{3,1,2,0:T(8,128)(2,1)} broadcast(bf16[512,3,256]{2,0,1:T(8,128)(2,1)S(1)} %copy-done.3), dimensions={1,2,3} | broadcast | bytes 7077888 | tf_op jit(solution)/shard_map/stack | solution.py:108
  39.3 4.9 %all-to-all-start.1 = ((bf16[8,512,3,256]{3,1,2,0:T(8,128)(2,1)}), bf16[8,512,3,256]{3,1,2,0:T(8,128)(2,1)}, u32[]{:S(2)}, u32[]{:S(2)}) async-start(bf16[8,512,3,256]{3,1,2,0:T(8,128)(2,1)} %stack.2), calls=%async_computation.1 | async-start | bytes 12582912 | tf_op jit(solution)/shard_map/all_to_all | solution.py:108
  44.3 0.7 all-gather.2.cloned.1.call-update
  45.2 0.8 multiply_cosine_fusion
  46.0 1.6 copy.146
  48.2 1.5 fusion.2
  49.7 75.1 %all-to-all-done.1 = bf16[8,512,3,256]{3,1,2,0:T(8,128)(2,1)} async-done(((bf16[8,512,3,256]{3,1,2,0:T(8,128)(2,1)}), bf16[8,512,3,256]{3,1,2,0:T(8,128)(2,1)}, u32[]{:S(2)}, u32[]{:S(2)}) %all-to-all-start.1) | async-done | bytes 6291488 | tf_op jit(solution)/shard_map/all_to_all | solution.py:108
  124.8 3.2 %copy.147 = bf16[8,512,3,256]{3,1,0,2:T(8,128)(2,1)S(1)} copy(bf16[8,512,3,256]{3,1,2,0:T(8,128)(2,1)} %all-to-all-done.1) | data formatting | bytes 12582912 | tf_op jit(solution)/shard_map/all_to_all | solution.py:108
  128.0 1.1 fusion.47
  129.3 0.8 subtract_convert_fusion
  130.7 0.6 pad_maximum_fusion
  131.5 1.1 broadcast_in_dim.96
  132.6 3.8 %all-to-all-start.2 = ((bf16[16,128,256]{2,1,0:T(8,128)(2,1)}), bf16[16,128,256]{2,1,0:T(8,128)(2,1)S(1)}, u32[]{:S(2)}, u32[]{:S(2)}) async-start(bf16[16,128,256]{2,1,0:T(8,128)(2,1)} %broadcast_in_dim.96), calls=%async_computation.2 | async-start | bytes 2097152 | tf_op jit(solution)/shard_map/all_to_all | solution.py:19
  137.0 1.5 concatenate.25
  138.5 1.5 concatenate.26
  140.0 1.5 concatenate.28
  141.5 1.5 concatenate.29
  142.9 1.6 copy.159
  144.5 1.6 copy.160
  146.1 1.6 copy.163
  147.6 1.6 copy.164
  149.2 1.8 select_reduce_fusion.1
  151.0 0.6 slice.46
  152.2 0.8 reshape.246
  153.0 1.0 fusion.23
  154.5 1.3 reshape.249
  155.8 1.5 convert_element_type.126
  157.3 1.2 convolution_bitcast_fusion
  158.5 0.7 copy.169
  159.2 1.6 copy.152
  160.7 1.4 reshape_reshape.3
  162.2 2.9 %select_reduce_fusion = (f32[2,32,64]{2,1,0:T(8,128)S(1)}, f32[2,32,64,128]{3,2,1,0:T(8,128)}) fusion(pred[2,128]{1,0:T(4,128)(4,1)S(1)} %copy-done.11, bf16[2,64,32,128]{3,2,1,0:T(8,128)(2,1)S(1)} %reshape_reshape.3, bf16[2,128,4096]{2,1,0:T(8,128)(2,1)S(1)} %copy-done), kind=kOutput, calls=%fused_computation.16 | convolution fusion | flops 135786496 | bytes 5259520 | tf_op jit(solution)/shard_map/mthd,mphd->mhtp/dot_general | solution.py:128
  165.3 2.5 %fusion.13 = f32[2,32,64]{2,1,0:T(8,128)S(1)} fusion(f32[2,32,64,128]{3,2,1,0:T(8,128)} %get-tuple-element.21, f32[2,32,64]{2,1,0:T(8,128)S(1)} %get-tuple-element.15, pred[2,128]{1,0:T(4,128)(4,1)S(1)} %copy-done.11), kind=kLoop, calls=%fused_computation.18 | loop fusion | flops 2093056 | bytes 2130176 | tf_op jit(solution)/shard_map/reduce_sum | solution.py:135
  168.1 0.6 copy.223
  168.7 7.2 %all-to-all-start.4 = ((bf16[16,2,128]{2,1,0:T(2,128)(2,1)}), bf16[16,2,128]{2,1,0:T(2,128)(2,1)S(1)}, u32[]{:S(2)}, u32[]{:S(2)}) async-start(bf16[16,2,128]{2,1,0:T(2,128)(2,1)} %bitcast.121), calls=%async_computation.4 | async-start | bytes 16384 | tf_op jit(solution)/shard_map/all_to_all | solution.py:179
  175.9 4.3 %fusion.10 = f32[2,64,32,128]{3,1,2,0:T(8,128)} fusion(f32[2,32,64,128]{3,2,1,0:T(8,128)} %get-tuple-element.21, f32[2,32,64]{2,1,0:T(8,128)S(1)} %get-tuple-element.15, pred[2,128]{1,0:T(4,128)(4,1)S(1)} %copy-done.11, bf16[2,128,4096]{2,1,0:T(8,128)(2,1)} %param.18), kind=kOutput, calls=%fused_computation.17 | convolution fusion | flops 136314880 | bytes 6308096 | tf_op jit(solution)/shard_map/mhtp,mphd->mthd/dot_general | solution.py:136
  181.1 2.8 %copy.156 = f32[2,64,32,128]{3,2,1,0:T(8,128)S(1)} copy(f32[2,64,32,128]{3,1,2,0:T(8,128)} %fusion.10) | data formatting | bytes 4194304 | tf_op jit(solution)/shard_map/mhtp,mphd->mthd/transpose | solution.py:136
  183.9 1.3 copy-done.1
  185.2 1.3 copy.225
  186.5 7.2 %all-to-all-start.5 = ((bf16[16,2,128]{2,1,0:T(2,128)(2,1)}), bf16[16,2,128]{2,1,0:T(2,128)(2,1)S(1)}, u32[]{:S(2)}, u32[]{:S(2)}) async-start(bf16[16,2,128]{2,1,0:T(2,128)(2,1)} %bitcast.120), calls=%async_computation.5 | async-start | bytes 16384 | tf_op jit(solution)/shard_map/all_to_all | solution.py:182
  193.8 2.0 bitcast_dynamic-update-slice_fusion
  195.8 1.8 convert_element_type.128
  197.6 1.4 copy.172
  199.0 2.3 all-to-all-done.5
  201.3 5.0 %all-to-all-start.3 = ((bf16[1,128,32,128]{3,1,0,2:T(8,128)(2,1)}), bf16[1,128,32,128]{3,1,0,2:T(8,128)(2,1)S(1)}, u32[]{:S(2)}, u32[]{:S(2)}) async-start(bf16[1,128,32,128]{3,1,0,2:T(8,128)(2,1)} %copy.172), calls=%async_computation.3 | async-start | bytes 2097152 | tf_op jit(solution)/shard_map/all_to_all | solution.py:189
  206.3 0.6 reshape.267
  206.9 0.7 copy.189
  208.2 1.2 reduce_max.35
  209.4 0.6 reshape.269
  210.0 0.7 copy.179
  210.7 1.3 fusion.36
  212.0 9.4 %all-to-all-done.3 = bf16[1,128,32,128]{3,1,0,2:T(8,128)(2,1)S(1)} async-done(((bf16[1,128,32,128]{3,1,0,2:T(8,128)(2,1)}), bf16[1,128,32,128]{3,1,0,2:T(8,128)(2,1)S(1)}, u32[]{:S(2)}, u32[]{:S(2)}) %all-to-all-start.3) | async-done | bytes 1048608 | tf_op jit(solution)/shard_map/all_to_all | solution.py:189
  221.5 1.4 fusion.9
  223.2 2.1 convolution_convert_fusion
  225.2 1.1 copy.219
  226.3 3.7 %all-to-all-start.6 = ((bf16[16,128,256]{2,1,0:T(8,128)(2,1)}), bf16[16,128,256]{2,1,0:T(8,128)(2,1)S(1)}, u32[]{:S(2)}, u32[]{:S(2)}) async-start(bf16[16,128,256]{2,1,0:T(8,128)(2,1)} %bitcast.128), calls=%async_computation.6 | async-start | bytes 2097152 | tf_op jit(solution)/shard_map/all_to_all | solution.py:33
  230.0 1.6 copy.186
  231.6 0.6 slice_bitcast_fusion
  232.2 13.7 %all-to-all-done.6 = bf16[16,128,256]{2,1,0:T(8,128)(2,1)S(1)} async-done(((bf16[16,128,256]{2,1,0:T(8,128)(2,1)}), bf16[16,128,256]{2,1,0:T(8,128)(2,1)S(1)}, u32[]{:S(2)}, u32[]{:S(2)}) %all-to-all-start.6) | async-done | bytes 1048608 | tf_op jit(solution)/shard_map/all_to_all | solution.py:33
  245.9 0.8 reduce_sum.62
  (63 shorter events, 5.7 us)
Async XLA Ops:
  7.2 155.0 %copy-start = (bf16[2,128,4096]{2,1,0:T(8,128)(2,1)S(1)}, bf16[2,128,4096]{2,1,0:T(8,128)(2,1)}, u32[]{:S(2)}) copy-start(bf16[2,128,4096]{2,1,0:T(8,128)(2,1)} %param.17) | copy-start | bytes 6291460
  9.5 26.5 %copy-start.3 = (bf16[512,3,256]{2,0,1:T(8,128)(2,1)S(1)}, bf16[512,3,256]{2,0,1:T(8,128)(2,1)}, u32[]{:S(2)}) copy-start(bf16[512,3,256]{2,0,1:T(8,128)(2,1)} %param.15) | copy-start | bytes 2359300
  39.3 5.6 %copy-start.9 = (f32[4096]{0:T(1024)S(1)}, f32[4096]{0:T(1024)}, u32[]{:S(2)}) copy-start(f32[4096]{0:T(1024)} %param.14) | copy-start | bytes 49156
  39.3 5.6 %copy-start.12 = (s32[2]{0:T(128)S(1)}, s32[2]{0:T(128)}, u32[]{:S(2)}) copy-start(s32[2]{0:T(128)} %param.19) | copy-start | bytes 28
  39.3 85.4 %all-to-all-start.1 = ((bf16[8,512,3,256]{3,1,2,0:T(8,128)(2,1)}), bf16[8,512,3,256]{3,1,2,0:T(8,128)(2,1)}, u32[]{:S(2)}, u32[]{:S(2)}) async-start(bf16[8,512,3,256]{3,1,2,0:T(8,128)(2,1)} %stack.2), calls=%async_computation.1 | async-start | bytes 12582912 | tf_op jit(solution)/shard_map/all_to_all | solution.py:108
  44.2 179.0 %all-gather.2.cloned.1.call-start = ((), (), s32[]{:S(2)}) async-start(), calls=%async_computation.7 | async-start | bytes 2359296 | tf_op jit(solution)/shard_map/all_gather | solution.py:110
  49.7 78.3 %copy-start.2 = (bf16[16,128,256]{1,2,0:T(8,128)(2,1)S(1)}, bf16[16,128,256]{1,2,0:T(8,128)(2,1)}, u32[]{:S(2)}) copy-start(bf16[16,128,256]{1,2,0:T(8,128)(2,1)} %fusion.2) | copy-start | bytes 3145732
  130.1 0.6 copy-start.5
  130.1 1.2 copy-start.6
  130.1 1.2 copy-start.7
  130.2 1.2 copy-start.8
  132.6 26.6 %all-to-all-start.2 = ((bf16[16,128,256]{2,1,0:T(8,128)(2,1)}), bf16[16,128,256]{2,1,0:T(8,128)(2,1)S(1)}, u32[]{:S(2)}, u32[]{:S(2)}) async-start(bf16[16,128,256]{2,1,0:T(8,128)(2,1)} %broadcast_in_dim.96), calls=%async_computation.2 | async-start | bytes 2097152 | tf_op jit(solution)/shard_map/all_to_all | solution.py:19
  159.2 3.0 %copy-start.11 = (pred[2,128]{1,0:T(4,128)(4,1)S(1)}, pred[2,128]{1,0:T(4,128)(4,1)}, u32[]{:S(2)}) copy-start(pred[2,128]{1,0:T(4,128)(4,1)} %broadcast_compare_fusion) | copy-start | bytes 772
  168.7 17.9 %all-to-all-start.4 = ((bf16[16,2,128]{2,1,0:T(2,128)(2,1)}), bf16[16,2,128]{2,1,0:T(2,128)(2,1)S(1)}, u32[]{:S(2)}, u32[]{:S(2)}) async-start(bf16[16,2,128]{2,1,0:T(2,128)(2,1)} %bitcast.121), calls=%async_computation.4 | async-start | bytes 16384 | tf_op jit(solution)/shard_map/all_to_all | solution.py:179
  175.9 4.3 %copy-start.10 = (f32[128,2]{0,1:T(2,128)S(1)}, f32[128,2]{0,1:T(2,128)}, u32[]{:S(2)}) copy-start(f32[128,2]{0,1:T(2,128)} %reshape.249) | copy-start | bytes 3076
  183.9 1.3 copy-start.1
  185.2 8.6 %copy-start.4 = (f32[2,64,2,128]{3,1,0,2:T(8,128)S(1)}, f32[2,64,2,128]{3,1,0,2:T(8,128)}, u32[]{:S(2)}) copy-start(f32[2,64,2,128]{3,1,0,2:T(8,128)} %copy.169) | copy-start | bytes 393220
  186.5 14.7 %all-to-all-start.5 = ((bf16[16,2,128]{2,1,0:T(2,128)(2,1)}), bf16[16,2,128]{2,1,0:T(2,128)(2,1)S(1)}, u32[]{:S(2)}, u32[]{:S(2)}) async-start(bf16[16,2,128]{2,1,0:T(2,128)(2,1)} %bitcast.120), calls=%async_computation.5 | async-start | bytes 16384 | tf_op jit(solution)/shard_map/all_to_all | solution.py:182
  201.3 20.2 %all-to-all-start.3 = ((bf16[1,128,32,128]{3,1,0,2:T(8,128)(2,1)}), bf16[1,128,32,128]{3,1,0,2:T(8,128)(2,1)S(1)}, u32[]{:S(2)}, u32[]{:S(2)}) async-start(bf16[1,128,32,128]{3,1,0,2:T(8,128)(2,1)} %copy.172), calls=%async_computation.3 | async-start | bytes 2097152 | tf_op jit(solution)/shard_map/all_to_all | solution.py:189
  226.3 19.6 %all-to-all-start.6 = ((bf16[16,128,256]{2,1,0:T(8,128)(2,1)}), bf16[16,128,256]{2,1,0:T(8,128)(2,1)S(1)}, u32[]{:S(2)}, u32[]{:S(2)}) async-start(bf16[16,128,256]{2,1,0:T(8,128)(2,1)} %bitcast.128), calls=%async_computation.6 | async-start | bytes 2097152 | tf_op jit(solution)/shard_map/all_to_all | solution.py:33
Sparse Core Ops, SparseCore 0:
  46.7 33.4 all-gather.1
